TPU v7x, 32 devices: a whole 2x2x4 slice. The times are simulated.
32 devices in a mesh: dp: 4 (over y, x), seq: 8 (over z, core).
Axes of the slice: x: 2, y: 2, z: 4, core: 2. Of those that a mesh axis runs over, the one named last changes fastest.
Arguments:
- queries: bfloat16 [4, 1024, 2048], P('dp', 'seq'), may hold values from -6 to 6
- key_vectors: bfloat16 [4, 1024, 2048], P('dp', 'seq'), may hold values from -6 to 6
- values: bfloat16 [4, 1024, 2048], P('dp', 'seq'), may hold values from -6 to 6
- out_grad: bfloat16 [4, 1024, 2048], P('dp', 'seq'), may hold values from -6 to 6
- inputs: bfloat16 [4, 1024, 2048], P('dp', 'seq'), may hold values from -6 to 6
Outputs:
- query_grad: bfloat16 [4, 1024, 2048], P('dp', 'seq')
- key_grad: bfloat16 [4, 1024, 2048], P('dp', 'seq')
- value_grad: bfloat16 [4, 1024, 2048], P('dp', 'seq')
- weight_grad: float32 [2048, 2048], P('dp', 'seq')
All inputs are finite; a program needn't handle non-finite values.
Results may differ from a plain program's by a relative error of at most 0.025.
Values may be sent and summed in bfloat16 or wider, within the bound.
No kernel may reach another device: no remote copies, remote signals or barrier semaphores. Data moves between devices by JAX's collectives and lax.ppermute only.
A program may use at most 128 MiB of HBM per device.

v0:
```python
import jax
import jax.numpy as jnp
from jax import lax
from jax.sharding import PartitionSpec as P

HD = 128


def partner(value, axis, apart):
    return lax.ppermute(value, axis, [(i, i ^ 1 << apart) for i in range(lax.axis_size(axis))])


def body(queries, key_vectors, values, out_grad, inputs):
    seq_count = lax.axis_size("seq")
    groups = seq_count // 2
    parity = lax.axis_index("seq") % 2
    is_even = parity == 0
    tok_rows = queries.shape[1]
    half_rows = tok_rows // 2
    width = queries.shape[2]
    group_width = 2 * width // seq_count
    heads_here = group_width // HD
    model_width = inputs.shape[2]
    own_rows = seq_count * half_rows
    length = 2 * own_rows
    doc_rows = own_rows // 4
    block_rows = min(doc_rows, max(256, length // 16))
    block_count = own_rows // block_rows
    scale = HD ** (-0.5)

    def to_heads(array):
        return (
            array[0]
            .reshape(half_rows, 2, groups, group_width)
            .transpose(0, 2, 1, 3)
            .reshape(half_rows, seq_count, group_width)
        )

    moved = (
        lax.all_to_all(to_heads(queries), "seq", split_axis=1, concat_axis=0, tiled=True),
        lax.all_to_all(to_heads(key_vectors), "seq", split_axis=1, concat_axis=0, tiled=True),
        lax.all_to_all(to_heads(values), "seq", split_axis=1, concat_axis=0, tiled=True),
        lax.all_to_all(to_heads(out_grad), "seq", split_axis=1, concat_axis=0, tiled=True),
    )
    q_rows = moved[0].reshape(own_rows, group_width)
    k_rows = moved[1].reshape(own_rows, group_width)
    v_rows = moved[2].reshape(own_rows, group_width)
    g_rows = moved[3].reshape(own_rows, group_width)
    k_other, v_other = partner((k_rows, v_rows), "seq", 0)

    def in_order(mine, theirs):
        even_rows = jnp.where(is_even, mine, theirs)
        odd_rows = jnp.where(is_even, theirs, mine)
        return jnp.stack([even_rows, odd_rows], axis=1).reshape(2 * mine.shape[0], mine.shape[1])

    key_all = in_order(k_rows, k_other).reshape(length, heads_here, HD)
    value_all = in_order(v_rows, v_other).reshape(length, heads_here, HD)
    query_heads = q_rows.reshape(own_rows, heads_here, HD)
    grad_heads = g_rows.reshape(own_rows, heads_here, HD)
    key_total = jnp.zeros((length, heads_here, HD), jnp.float32)
    value_total = jnp.zeros((length, heads_here, HD), jnp.float32)
    query_parts = []
    for block in range(block_count):
        start = block * block_rows
        stop = start + block_rows
        low = 2 * (start // doc_rows * doc_rows)
        high = 2 * stop
        query_block = query_heads[start:stop]
        grad_block = grad_heads[start:stop]
        key_block = key_all[low:high]
        value_block = value_all[low:high]
        scores = (
            jnp.einsum("qhd,khd->hqk", query_block, key_block, preferred_element_type=jnp.float32)
            * scale
        )
        query_pos = 2 * (start + jnp.arange(block_rows, dtype=jnp.int32)) + parity
        key_pos = low + jnp.arange(high - low, dtype=jnp.int32)
        visible = key_pos[None, :] <= query_pos[:, None]
        scores = jnp.where(visible[None], scores, -jnp.inf)
        top = jnp.max(scores, axis=2, keepdims=True)
        weights = jnp.exp(scores - top)
        probs = weights / jnp.sum(weights, axis=2, keepdims=True)
        probs_low = probs.astype(jnp.bfloat16)
        dprob = jnp.einsum(
            "qhd,khd->hqk", grad_block, value_block, preferred_element_type=jnp.float32
        )
        delta = jnp.sum(probs * dprob, axis=2, keepdims=True)
        dscore = (probs * (dprob - delta) * scale).astype(jnp.bfloat16)
        query_parts.append(
            jnp.einsum(
                "hqk,khd->qhd", dscore, key_block, preferred_element_type=jnp.float32
            ).astype(jnp.bfloat16)
        )
        key_total = key_total.at[low:high].add(
            jnp.einsum("hqk,qhd->khd", dscore, query_block, preferred_element_type=jnp.float32)
        )
        value_total = value_total.at[low:high].add(
            jnp.einsum("hqk,qhd->khd", probs_low, grad_block, preferred_element_type=jnp.float32)
        )
    query_grad = jnp.concatenate(query_parts, axis=0).reshape(own_rows, group_width)

    def by_parity(total):
        paired = total.reshape(own_rows, 2, group_width)
        mine = jnp.where(is_even, paired[:, 0], paired[:, 1])
        theirs = jnp.where(is_even, paired[:, 1], paired[:, 0])
        return (mine.astype(jnp.bfloat16), theirs.astype(jnp.bfloat16))

    key_mine, key_theirs = by_parity(key_total)
    value_mine, value_theirs = by_parity(value_total)
    key_back, value_back = partner((key_theirs, value_theirs), "seq", 0)
    key_grad = (key_mine.astype(jnp.float32) + key_back.astype(jnp.float32)).astype(jnp.bfloat16)
    value_grad = (value_mine.astype(jnp.float32) + value_back.astype(jnp.float32)).astype(
        jnp.bfloat16
    )
    spread = jnp.broadcast_to(
        inputs[0].reshape(half_rows, 1, 2, model_width), (half_rows, groups, 2, model_width)
    ).reshape(half_rows, seq_count, model_width)
    input_rows = lax.all_to_all(spread, "seq", split_axis=1, concat_axis=0, tiled=True).reshape(
        own_rows, model_width
    )
    term = jnp.einsum("td,tc->dc", input_rows, value_grad, preferred_element_type=jnp.float32)
    halves = term.reshape(term.shape[0], 2, term.shape[1] // 2)
    mine = jnp.where(is_even, halves[:, 0], halves[:, 1])
    theirs = jnp.where(is_even, halves[:, 1], halves[:, 0])
    mine, theirs = (mine, theirs)
    received = partner(theirs.astype(jnp.bfloat16), "seq", 0).astype(theirs.dtype)
    weight_grad = lax.psum_scatter(
        (mine + received).astype(jnp.bfloat16), "dp", scatter_dimension=0, tiled=True
    ).astype(jnp.float32)

    def to_tokens(array):
        return array.reshape(seq_count, half_rows, 1, group_width)

    def from_heads(array):
        return (
            array.reshape(half_rows, groups, 2, group_width)
            .transpose(0, 2, 1, 3)
            .reshape(1, tok_rows, width)
        )

    returned = (
        lax.all_to_all(to_tokens(query_grad), "seq", split_axis=0, concat_axis=2, tiled=True),
        lax.all_to_all(to_tokens(key_grad), "seq", split_axis=0, concat_axis=2, tiled=True),
        lax.all_to_all(to_tokens(value_grad), "seq", split_axis=0, concat_axis=2, tiled=True),
    )
    return (from_heads(returned[0]), from_heads(returned[1]), from_heads(returned[2]), weight_grad)


def solution(mesh):
    return jax.shard_map(
        body,
        mesh=mesh,
        in_specs=(
            P("dp", "seq", None),
            P("dp", "seq", None),
            P("dp", "seq", None),
            P("dp", "seq", None),
            P("dp", "seq", None),
        ),
        out_specs=(
            P("dp", "seq", None),
            P("dp", "seq", None),
            P("dp", "seq", None),
            P("dp", "seq"),
        ),
        check_vma=False,
    )
```

profile of v0, /device:TPU:0, one launch (start us, length us, event | category | flops | bytes accessed | tf_op | source)
XLA Modules:
  0.0 255.6 jit_solution(17739342030090548654)
XLA Ops:
  9.6 6.5 %all-to-all-start.2 = ((bf16[64,8,512]{2,0,1:T(8,128)(2,1)}), bf16[64,8,512]{2,0,1:T(8,128)(2,1)S(1)}, u32[]{:S(2)}, u32[]{:S(2)}) async-start(bf16[64,8,512]{2,0,1:T(8,128)(2,1)} %bitcast.15), calls=%async_computation.2 | async-start | bytes 1048576 | tf_op jit(solution)/shard_map/all_to_all | solution.py:42
  17.4 14.0 %all-to-all-done.2 = bf16[64,8,512]{2,0,1:T(8,128)(2,1)S(1)} async-done(((bf16[64,8,512]{2,0,1:T(8,128)(2,1)}), bf16[64,8,512]{2,0,1:T(8,128)(2,1)S(1)}, u32[]{:S(2)}, u32[]{:S(2)}) %all-to-all-start.2) | async-done | bytes 524320 | tf_op jit(solution)/shard_map/all_to_all | solution.py:42
  31.4 3.6 %all-to-all-start.3 = ((bf16[64,8,512]{2,0,1:T(8,128)(2,1)}), bf16[64,8,512]{2,0,1:T(8,128)(2,1)S(1)}, u32[]{:S(2)}, u32[]{:S(2)}) async-start(bf16[64,8,512]{2,0,1:T(8,128)(2,1)} %bitcast.24), calls=%async_computation.3 | async-start | bytes 1048576 | tf_op jit(solution)/shard_map/all_to_all | solution.py:43
  36.4 13.9 %all-to-all-done.3 = bf16[64,8,512]{2,0,1:T(8,128)(2,1)S(1)} async-done(((bf16[64,8,512]{2,0,1:T(8,128)(2,1)}), bf16[64,8,512]{2,0,1:T(8,128)(2,1)S(1)}, u32[]{:S(2)}, u32[]{:S(2)}) %all-to-all-start.3) | async-done | bytes 524320 | tf_op jit(solution)/shard_map/all_to_all | solution.py:43
  50.4 3.5 %all-to-all-start = ((bf16[64,8,512]{2,0,1:T(8,128)(2,1)}), bf16[64,8,512]{2,0,1:T(8,128)(2,1)S(1)}, u32[]{:S(2)}, u32[]{:S(2)}) async-start(bf16[64,8,512]{2,0,1:T(8,128)(2,1)} %bitcast.1), calls=%async_computation | async-start | bytes 1048576 | tf_op jit(solution)/shard_map/all_to_all | solution.py:41
  55.9 13.2 %all-to-all-done = bf16[64,8,512]{2,0,1:T(8,128)(2,1)S(1)} async-done(((bf16[64,8,512]{2,0,1:T(8,128)(2,1)}), bf16[64,8,512]{2,0,1:T(8,128)(2,1)S(1)}, u32[]{:S(2)}, u32[]{:S(2)}) %all-to-all-start) | async-done | bytes 524320 | tf_op jit(solution)/shard_map/all_to_all | solution.py:41
  69.1 3.5 %all-to-all-start.1 = ((bf16[64,8,512]{2,0,1:T(8,128)(2,1)}), bf16[64,8,512]{2,0,1:T(8,128)(2,1)S(1)}, u32[]{:S(2)}, u32[]{:S(2)}) async-start(bf16[64,8,512]{2,0,1:T(8,128)(2,1)} %bitcast.10), calls=%async_computation.1 | async-start | bytes 1048576 | tf_op jit(solution)/shard_map/all_to_all | solution.py:40
  77.6 10.3 %all-to-all-done.1 = bf16[64,8,512]{2,0,1:T(8,128)(2,1)S(1)} async-done(((bf16[64,8,512]{2,0,1:T(8,128)(2,1)}), bf16[64,8,512]{2,0,1:T(8,128)(2,1)S(1)}, u32[]{:S(2)}, u32[]{:S(2)}) %all-to-all-start.1) | async-done | bytes 524320 | tf_op jit(solution)/shard_map/all_to_all | solution.py:40
  89.5 3.8 %all-to-all-start.7 = ((bf16[64,8,2048]{2,0,1:T(8,128)(2,1)}), bf16[64,8,2048]{2,0,1:T(8,128)(2,1)S(1)}, u32[]{:S(2)}, u32[]{:S(2)}) async-start(bf16[64,8,2048]{2,0,1:T(8,128)(2,1)} %bitcast.65), calls=%async_computation.7 | async-start | bytes 4194304 | tf_op jit(solution)/shard_map/all_to_all | solution.py:118
  114.6 2.5 scatter-add.34
  121.4 2.4 fusion.17
  126.1 2.4 fusion.24
  133.6 2.5 fusion.26
  136.2 3.9 %copy.167 = bf16[1024,4,128]{2,1,0:T(4,128)(2,1)} copy(f32[1024,4,128]{2,0,1:T(8,128)} %fusion.26) | data formatting | bytes 3145728 | tf_op jit(solution)/shard_map/scatter-add | solution.py:97
  141.6 3.0 %fusion.60 = (bf16[512,1,512]{2,1,0:T(2,128)(2,1)S(1)}, f32[512,1,512]{2,1,0:T(1,128)}) fusion(pred[]{:T(512)S(6)} %eq.5, bf16[512,2,512]{2,1,0:T(2,128)(2,1)S(1)} %reshape.498), kind=kLoop, calls=%fused_computation.98 | loop fusion | flops 786432 | bytes 2621441 | tf_op jit(solution)/shard_map/convert_element_type | solution.py:106
  146.0 2.4 fusion.54
  150.4 2.7 %fusion.53 = bf16[128,4,128]{2,0,1:T(8,128)(2,1)} fusion(f32[4,128,256]{1,2,0:T(8,128)} %convolution_bitcast_fusion.9, bf16[256,4,128]{2,1,0:T(4,128)(2,1)} %copy-done.18, f32[4,128,256]{1,2,0:T(8,128)} %get-tuple-element.129, f32[4,128]{1,0:T(4,128)S(1)} %get-tuple-element.128), kind=kOutput, calls=%fused_computation.91 | convolution fusion | flops 34538240 | bytes 1443840 | tf_op jit(solution)/shard_map/hqk,khd->qhd/dot_general | solution.py:90
  154.2 2.7 %fusion.52 = bf16[128,4,128]{2,0,1:T(8,128)(2,1)} fusion(f32[4,128,256]{1,2,0:T(8,128)} %convolution_bitcast_fusion.10, bf16[256,4,128]{2,1,0:T(4,128)(2,1)} %slice.311, f32[4,128,256]{1,2,0:T(8,128)} %get-tuple-element.131, f32[4,128]{1,0:T(4,128)S(1)} %get-tuple-element.130), kind=kOutput, calls=%fused_computation.90 | convolution fusion | flops 34538240 | bytes 1443840 | tf_op jit(solution)/shard_map/hqk,khd->qhd/dot_general | solution.py:90
  160.3 2.4 convolution_bitcast_fusion.7
  162.7 2.6 %scatter-add.26 = f32[1024,4,128]{2,0,1:T(8,128)} pad(f32[256,4,128]{2,0,1:T(8,128)} %convolution_bitcast_fusion.7, f32[]{:T(128)} %constant.216.clone.1), padding=0_768x0_0x0_0 | pad | bytes 2621444 | tf_op jit(solution)/shard_map/scatter-add | solution.py:94
  165.3 2.8 %fusion.18 = f32[1024,4,128]{2,0,1:T(8,128)} fusion(f32[1024,4,128]{2,0,1:T(8,128)} %scatter-add.26, f32[4,128,256]{1,2,0:T(8,128)} %convolution_bitcast_fusion.10, bf16[128,4,128]{2,1,0:T(4,128)(2,1)S(1)} %copy-done.23, f32[4,128,256]{1,2,0:T(8,128)} %get-tuple-element.131, f32[4,128]{1,0:T(4,128)S(1)} %get-tuple-element.130), kind=kOutput, calls=%fused_computation.43 | convolution fusion | flops 34472704 | bytes 2756608 | tf_op jit(solution)/shard_map/hqk,qhd->khd/dot_general | solution.py:95
  170.1 4.8 %all-to-all-start.4 = ((bf16[8,64,1,512]{3,1,2,0:T(8,128)(2,1)}), bf16[8,64,1,512]{3,1,2,0:T(8,128)(2,1)}, u32[]{:S(2)}, u32[]{:S(2)}) async-start(bf16[8,64,1,512]{3,1,2,0:T(8,128)(2,1)} %bitcast.239), calls=%async_computation.4 | async-start | bytes 1048576 | tf_op jit(solution)/shard_map/all_to_all | solution.py:142
  174.9 2.3 fusion.241
  181.4 2.9 %copy.181 = f32[2048,1,256]{2,0,1:T(8,128)} copy(f32[2048,1,256]{0,2,1:T(8,128)} %get-tuple-element.100) | data formatting | bytes 4194304
  187.7 2.8 %fusion.20 = f32[1024,4,128]{2,0,1:T(8,128)} fusion(f32[1024,4,128]{2,0,1:T(8,128)} %fusion.18, f32[4,128,256]{1,2,0:T(8,128)} %convolution_bitcast_fusion.9, bf16[128,4,128]{2,1,0:T(4,128)(2,1)S(1)} %copy-done.22, f32[4,128,256]{1,2,0:T(8,128)} %get-tuple-element.129, f32[4,128]{1,0:T(4,128)S(1)} %get-tuple-element.128), kind=kOutput, calls=%fused_computation.50 | convolution fusion | flops 34603776 | bytes 3280896 | tf_op jit(solution)/shard_map/hqk,qhd->khd/dot_general | solution.py:95
  190.5 2.8 %fusion.22 = f32[1024,4,128]{2,0,1:T(8,128)} fusion(f32[1024,4,128]{2,0,1:T(8,128)} %fusion.20, f32[4,128,256]{1,2,0:T(8,128)} %copy-done.7, bf16[128,4,128]{2,1,0:T(4,128)(2,1)S(1)} %copy-done.20, f32[4,128,256]{1,2,0:T(8,128)} %get-tuple-element.127, f32[4,128]{1,0:T(4,128)S(1)} %get-tuple-element.126), kind=kOutput, calls=%fused_computation.52 | convolution fusion | flops 34603776 | bytes 3280896 | tf_op jit(solution)/shard_map/hqk,qhd->khd/dot_general | solution.py:95
  193.3 3.9 %copy.160 = bf16[1024,4,128]{2,1,0:T(4,128)(2,1)} copy(f32[1024,4,128]{2,0,1:T(8,128)} %fusion.22) | data formatting | bytes 3145728 | tf_op jit(solution)/shard_map/scatter-add | solution.py:94
  198.7 3.0 %fusion.57 = (bf16[512,1,512]{2,1,0:T(2,128)(2,1)S(1)}, f32[512,1,512]{2,1,0:T(1,128)}) fusion(pred[]{:T(512)S(6)} %eq.5, bf16[512,2,512]{2,1,0:T(2,128)(2,1)S(1)} %reshape.494), kind=kLoop, calls=%fused_computation.95 | loop fusion | flops 786432 | bytes 2621441 | tf_op jit(solution)/shard_map/convert_element_type | solution.py:106
  202.7 2.7 %fusion.8 = bf16[2048,256]{1,0:T(8,128)(2,1)} fusion(bf16[2048,256]{1,0:T(8,128)(2,1)} %collective-permute-done.4, f32[2048,1,256]{2,0,1:T(8,128)S(1)} %copy-done, f32[2048,1,256]{2,0,1:T(8,128)S(1)} %copy.182, pred[]{:T(512)S(6)} %eq.5), kind=kLoop, calls=%fused_computation.9 | loop fusion | flops 2097152 | bytes 6291457 | tf_op jit(solution)/shard_map/convert_element_type | solution.py:128
  206.7 19.9 %all_to_all.120 = bf16[8,64,1,512]{3,1,2,0:T(8,128)(2,1)S(1)} all-to-all(bf16[8,64,1,512]{3,1,2,0:T(8,128)(2,1)S(1)} %bitcast.248), channel_id=1, replica_groups=mesh['dp'=4,'seq'=8] {'seq'}, dimensions={0} | all-to-all | bytes 1048576 | tf_op jit(solution)/shard_map/all_to_all | solution.py:143
  226.6 3.8 %all-to-all-start.6 = ((bf16[8,64,1,512]{3,1,2,0:T(8,128)(2,1)}), bf16[8,64,1,512]{3,1,2,0:T(8,128)(2,1)S(1)}, u32[]{:S(2)}, u32[]{:S(2)}) async-start(bf16[8,64,1,512]{3,1,2,0:T(8,128)(2,1)} %bitcast.60), calls=%async_computation.6 | async-start | bytes 1048576 | tf_op jit(solution)/shard_map/all_to_all | solution.py:144
  234.6 10.8 %all-to-all-done.6 = bf16[8,64,1,512]{3,1,2,0:T(8,128)(2,1)S(1)} async-done(((bf16[8,64,1,512]{3,1,2,0:T(8,128)(2,1)}), bf16[8,64,1,512]{3,1,2,0:T(8,128)(2,1)S(1)}, u32[]{:S(2)}, u32[]{:S(2)}) %all-to-all-start.6) | async-done | bytes 524320 | tf_op jit(solution)/shard_map/all_to_all | solution.py:144
  (150 shorter events, 76.6 us)
Async XLA Ops:
  7.2 8.9 %copy-start.12 = (bf16[1,128,2048]{2,1,0:T(8,128)(2,1)S(1)}, bf16[1,128,2048]{2,1,0:T(8,128)(2,1)}, u32[]{:S(2)}) copy-start(bf16[1,128,2048]{2,1,0:T(8,128)(2,1)} %param.24) | copy-start | bytes 1572868
  9.6 25.5 %copy-start.13 = (bf16[1,128,2048]{2,1,0:T(8,128)(2,1)S(1)}, bf16[1,128,2048]{2,1,0:T(8,128)(2,1)}, u32[]{:S(2)}) copy-start(bf16[1,128,2048]{2,1,0:T(8,128)(2,1)} %param.22) | copy-start | bytes 1572868
  9.6 21.8 %all-to-all-start.2 = ((bf16[64,8,512]{2,0,1:T(8,128)(2,1)}), bf16[64,8,512]{2,0,1:T(8,128)(2,1)S(1)}, u32[]{:S(2)}, u32[]{:S(2)}) async-start(bf16[64,8,512]{2,0,1:T(8,128)(2,1)} %bitcast.15), calls=%async_computation.2 | async-start | bytes 1048576 | tf_op jit(solution)/shard_map/all_to_all | solution.py:42
  31.4 22.4 %copy-start.14 = (bf16[1,128,2048]{2,1,0:T(8,128)(2,1)S(1)}, bf16[1,128,2048]{2,1,0:T(8,128)(2,1)}, u32[]{:S(2)}) copy-start(bf16[1,128,2048]{2,1,0:T(8,128)(2,1)} %param.21) | copy-start | bytes 1572868
  31.4 18.9 %all-to-all-start.3 = ((bf16[64,8,512]{2,0,1:T(8,128)(2,1)}), bf16[64,8,512]{2,0,1:T(8,128)(2,1)S(1)}, u32[]{:S(2)}, u32[]{:S(2)}) async-start(bf16[64,8,512]{2,0,1:T(8,128)(2,1)} %bitcast.24), calls=%async_computation.3 | async-start | bytes 1048576 | tf_op jit(solution)/shard_map/all_to_all | solution.py:43
  50.4 18.8 %all-to-all-start = ((bf16[64,8,512]{2,0,1:T(8,128)(2,1)}), bf16[64,8,512]{2,0,1:T(8,128)(2,1)S(1)}, u32[]{:S(2)}, u32[]{:S(2)}) async-start(bf16[64,8,512]{2,0,1:T(8,128)(2,1)} %bitcast.1), calls=%async_computation | async-start | bytes 1048576 | tf_op jit(solution)/shard_map/all_to_all | solution.py:41
  69.1 18.8 %all-to-all-start.1 = ((bf16[64,8,512]{2,0,1:T(8,128)(2,1)}), bf16[64,8,512]{2,0,1:T(8,128)(2,1)S(1)}, u32[]{:S(2)}, u32[]{:S(2)}) async-start(bf16[64,8,512]{2,0,1:T(8,128)(2,1)} %bitcast.10), calls=%async_computation.1 | async-start | bytes 1048576 | tf_op jit(solution)/shard_map/all_to_all | solution.py:40
  74.1 30.5 %collective-permute-start = (bf16[512,512]{1,0:T(8,128)(2,1)S(1)}, bf16[512,512]{1,0:T(8,128)(2,1)}, u32[]{:S(2)}, u32[]{:S(2)}) collective-permute-start(bf16[512,512]{1,0:T(8,128)(2,1)S(1)} %bitcast.238), channel_id=1, source_target_pairs={{0,1},{1,0},{2,3},{3,2},{4,5},{5,4},{6,7},{7,6},{8,9},{9,8},{10,11... | collective-permute-start | bytes 1572872 | tf_op jit(solution)/shard_map/ppermute | solution.py:10
  76.6 51.8 %collective-permute-start.1 = (bf16[512,512]{1,0:T(8,128)(2,1)S(1)}, bf16[512,512]{1,0:T(8,128)(2,1)}, u32[]{:S(2)}, u32[]{:S(2)}) collective-permute-start(bf16[512,512]{1,0:T(8,128)(2,1)S(1)} %bitcast.237), channel_id=1, source_target_pairs={{0,1},{1,0},{2,3},{3,2},{4,5},{5,4},{6,7},{7,6},{8,9},{9,8},{10,11... | collective-permute-start | bytes 1572872 | tf_op jit(solution)/shard_map/ppermute | solution.py:10
  89.5 80.6 %all-to-all-start.7 = ((bf16[64,8,2048]{2,0,1:T(8,128)(2,1)}), bf16[64,8,2048]{2,0,1:T(8,128)(2,1)S(1)}, u32[]{:S(2)}, u32[]{:S(2)}) async-start(bf16[64,8,2048]{2,0,1:T(8,128)(2,1)} %bitcast.65), calls=%async_computation.7 | async-start | bytes 4194304 | tf_op jit(solution)/shard_map/all_to_all | solution.py:118
  110.1 6.9 %copy-start.15 = (bf16[256,4,128]{2,1,0:T(4,128)(2,1)}, bf16[256,4,128]{2,1,0:T(4,128)(2,1)S(1)}, u32[]{:S(2)}) copy-start(bf16[256,4,128]{2,1,0:T(4,128)(2,1)S(1)} %slice.303) | copy-start | bytes 786436
  112.3 4.8 %copy-start.19 = (bf16[128,4,128]{2,1,0:T(4,128)(2,1)S(1)}, bf16[128,4,128]{2,1,0:T(4,128)(2,1)}, u32[]{:S(2)}) copy-start(bf16[128,4,128]{2,1,0:T(4,128)(2,1)} %slice.329) | copy-start | bytes 393220
  117.1 4.3 %copy-start.9 = (bf16[128,4,128]{2,1,0:T(4,128)(2,1)S(1)}, bf16[128,4,128]{2,1,0:T(4,128)(2,1)}, u32[]{:S(2)}) copy-start(bf16[128,4,128]{2,1,0:T(4,128)(2,1)} %slice.317) | copy-start | bytes 393220
  121.4 4.7 %copy-start.11 = (bf16[128,4,128]{2,1,0:T(4,128)(2,1)S(1)}, bf16[128,4,128]{2,1,0:T(4,128)(2,1)}, u32[]{:S(2)}) copy-start(bf16[128,4,128]{2,1,0:T(4,128)(2,1)} %slice.325) | copy-start | bytes 393220
  124.2 4.3 %copy-start.18 = (bf16[256,4,128]{2,1,0:T(4,128)(2,1)}, bf16[256,4,128]{2,1,0:T(4,128)(2,1)S(1)}, u32[]{:S(2)}) copy-start(bf16[256,4,128]{2,1,0:T(4,128)(2,1)S(1)} %slice.319) | copy-start | bytes 786436
  141.5 4.2 %copy-start.6 = (bf16[256,4,128]{2,1,0:T(4,128)(2,1)S(1)}, bf16[256,4,128]{2,1,0:T(4,128)(2,1)}, u32[]{:S(2)}) copy-start(bf16[256,4,128]{2,1,0:T(4,128)(2,1)} %slice.331) | copy-start | bytes 786436
  145.5 22.5 %collective-permute-start.3 = (bf16[512,512]{1,0:T(8,128)(2,1)}, bf16[512,512]{1,0:T(8,128)(2,1)}, u32[]{:S(2)}, u32[]{:S(2)}) collective-permute-start(bf16[512,512]{1,0:T(8,128)(2,1)} %bitcast.233), channel_id=1, source_target_pairs={{0,1},{1,0},{2,3},{3,2},{4,5},{5,4},{6,7},{7,6},{8,9},{9,8},{10,11... | collective-permute-start | bytes 1572872 | tf_op jit(solution)/shard_map/ppermute | solution.py:10
  146.0 7.2 %copy-start.7 = (f32[4,128,256]{1,2,0:T(8,128)}, f32[4,128,256]{1,2,0:T(8,128)S(1)}, u32[]{:S(2)}) copy-start(f32[4,128,256]{1,2,0:T(8,128)S(1)} %convolution_bitcast_fusion.8) | copy-start | bytes 1572868
  148.5 4.7 %copy-start.4 = (bf16[256,4,128]{2,1,0:T(4,128)(2,1)S(1)}, bf16[256,4,128]{2,1,0:T(4,128)(2,1)}, u32[]{:S(2)}) copy-start(bf16[256,4,128]{2,1,0:T(4,128)(2,1)} %slice.315) | copy-start | bytes 786436
  148.5 4.7 %copy-start.10 = (bf16[128,4,128]{2,1,0:T(4,128)(2,1)S(1)}, bf16[128,4,128]{2,1,0:T(4,128)(2,1)}, u32[]{:S(2)}) copy-start(bf16[128,4,128]{2,1,0:T(4,128)(2,1)} %slice.317) | copy-start | bytes 393220
  153.2 3.8 %copy-start.8 = (bf16[128,4,128]{2,1,0:T(4,128)(2,1)S(1)}, bf16[128,4,128]{2,1,0:T(4,128)(2,1)}, u32[]{:S(2)}) copy-start(bf16[128,4,128]{2,1,0:T(4,128)(2,1)} %slice.309) | copy-start | bytes 393220
  154.2 3.0 %copy-start.16 = (bf16[256,4,128]{2,1,0:T(4,128)(2,1)S(1)}, bf16[256,4,128]{2,1,0:T(4,128)(2,1)}, u32[]{:S(2)}) copy-start(bf16[256,4,128]{2,1,0:T(4,128)(2,1)} %copy-done.15) | copy-start | bytes 786436
  160.3 5.0 %copy-start.23 = (bf16[128,4,128]{2,1,0:T(4,128)(2,1)S(1)}, bf16[128,4,128]{2,1,0:T(4,128)(2,1)}, u32[]{:S(2)}) copy-start(bf16[128,4,128]{2,1,0:T(4,128)(2,1)} %slice.313) | copy-start | bytes 393220
  162.7 5.4 %copy-start.1 = (f32[512,1,512]{2,1,0:T(1,128)S(1)}, f32[512,1,512]{2,1,0:T(1,128)}, u32[]{:S(2)}) copy-start(f32[512,1,512]{2,1,0:T(1,128)} %get-tuple-element.103) | copy-start | bytes 3145732
  170.1 36.5 %all-to-all-start.4 = ((bf16[8,64,1,512]{3,1,2,0:T(8,128)(2,1)}), bf16[8,64,1,512]{3,1,2,0:T(8,128)(2,1)}, u32[]{:S(2)}, u32[]{:S(2)}) async-start(bf16[8,64,1,512]{3,1,2,0:T(8,128)(2,1)} %bitcast.239), calls=%async_computation.4 | async-start | bytes 1048576 | tf_op jit(solution)/shard_map/all_to_all | solution.py:142
  174.9 72.1 %reduce-scatter.2.cloned.1.call-start = ((), (), s32[]{:S(2)}) async-start(), calls=%async_computation.9 | async-start | bytes 1310720 | tf_op jit(solution)/shard_map/reduce_scatter | solution.py:127
  184.4 3.3 %copy-start.22 = (bf16[128,4,128]{2,1,0:T(4,128)(2,1)S(1)}, bf16[128,4,128]{2,1,0:T(4,128)(2,1)}, u32[]{:S(2)}) copy-start(bf16[128,4,128]{2,1,0:T(4,128)(2,1)} %slice.321) | copy-start | bytes 393220
  185.6 4.9 %copy-start.20 = (bf16[128,4,128]{2,1,0:T(4,128)(2,1)S(1)}, bf16[128,4,128]{2,1,0:T(4,128)(2,1)}, u32[]{:S(2)}) copy-start(bf16[128,4,128]{2,1,0:T(4,128)(2,1)} %slice.329) | copy-start | bytes 393220
  185.6 17.1 %collective-permute-start.4 = (bf16[2048,256]{1,0:T(8,128)(2,1)}, bf16[2048,256]{1,0:T(8,128)(2,1)}, u32[]{:S(2)}, u32[]{:S(2)}) collective-permute-start(bf16[2048,256]{1,0:T(8,128)(2,1)} %fusion.61), channel_id=1, source_target_pairs={{0,1},{1,0},{2,3},{3,2},{4,5},{5,4},{6,7},{7,6},{8,9},{9,8},{10,11... | collective-permute-start | bytes 3145736 | tf_op jit(solution)/shard_map/ppermute | solution.py:10
  198.7 3.9 %copy-start = (f32[2048,1,256]{2,0,1:T(8,128)S(1)}, f32[2048,1,256]{2,0,1:T(8,128)}, u32[]{:S(2)}) copy-start(f32[2048,1,256]{2,0,1:T(8,128)} %copy.181) | copy-start | bytes 6291460
  202.7 2.8 %collective-permute-start.2 = (bf16[512,512]{1,0:T(8,128)(2,1)}, bf16[512,512]{1,0:T(8,128)(2,1)}, u32[]{:S(2)}, u32[]{:S(2)}) collective-permute-start(bf16[512,512]{1,0:T(8,128)(2,1)} %bitcast.234), channel_id=1, source_target_pairs={{0,1},{1,0},{2,3},{3,2},{4,5},{5,4},{6,7},{7,6},{8,9},{9,8},{10,11... | collective-permute-start | bytes 1572872 | tf_op jit(solution)/shard_map/ppermute | solution.py:10
  226.6 18.8 %all-to-all-start.6 = ((bf16[8,64,1,512]{3,1,2,0:T(8,128)(2,1)}), bf16[8,64,1,512]{3,1,2,0:T(8,128)(2,1)S(1)}, u32[]{:S(2)}, u32[]{:S(2)}) async-start(bf16[8,64,1,512]{3,1,2,0:T(8,128)(2,1)} %bitcast.60), calls=%async_computation.6 | async-start | bytes 1048576 | tf_op jit(solution)/shard_map/all_to_all | solution.py:144
  (9 other events, 18.4 us)
Sparse Core Ops, SparseCore 0:
  205.5 28.9 reduce-scatter.1
where the time goes:
time: 258 us; the launch traced here: 256 us
  waiting for transfers between devices  62.4 us (24%)
  local copies, waits for them, and re-layouts  61.6 us (24%)
  matrix products  44 us (17%)
  starting transfers between devices  32.3 us (13%)
  other arithmetic  21 us (8%)
  blocking collectives  19.9 us (8%)
  between operations  14.5 us (6%)
    all_to_all x1, blocking collectives, body(): lax.all_to_all(to_tokens(key_grad), 'seq', split_axis=0, concat_axis=2, t...  19.9 us
    all_to_all x1, waiting for transfers between devices, body(): lax.all_to_all(to_heads(values), 'seq', split_axis=1, concat_axis=0, tile...  14 us
    all_to_all x1, waiting for transfers between devices, body(): lax.all_to_all(to_heads(out_grad), 'seq', split_axis=1, concat_axis=0, ti...  13.9 us
    all_to_all x1, waiting for transfers between devices, body(): lax.all_to_all(to_heads(key_vectors), 'seq', split_axis=1, concat_axis=0,...  13.2 us
    dot_general x4, matrix products, body(): jnp.einsum('hqk,qhd->khd', dscore, query_block, preferred_element_type=jn...  10.8 us
    all_to_all x1, waiting for transfers between devices, body(): lax.all_to_all(to_tokens(value_grad), 'seq', split_axis=0, concat_axis=2,...  10.8 us
    all_to_all x1, waiting for transfers between devices, body(): lax.all_to_all(to_heads(queries), 'seq', split_axis=1, concat_axis=0, til...  10.3 us
    dot_general x4, matrix products, body(): jnp.einsum('hqk,qhd->khd', probs_low, grad_block, preferred_element_type=...  9.58 us
  transfers between devices with their start and end apart: 13, of which 5 were waited for; matrix products, arithmetic and copies ran while one was open for 48% of the time, Pallas kernels for 0%

commit v1 on v0

--- a/solution.py
+++ b/solution.py
@@ -4,6 +4,28 @@
 from jax.sharding import PartitionSpec as P
 
 HD = 128
+
+
+def cut_along(x, dim, peers):
+    before, after = (x.shape[:dim], x.shape[dim + 1 :])
+    return jnp.moveaxis(x.reshape(*before, peers, -1, *after), dim, 0)
+
+
+def joined_along(blocks, dim):
+    dims = list(blocks.shape[1:])
+    dims[dim] *= blocks.shape[0]
+    return jnp.moveaxis(blocks, 0, dim).reshape(dims)
+
+
+def pairwise_exchange(x, axis, split_dim, concat_dim):
+    devices, index = (lax.axis_size(axis), lax.axis_index(axis))
+    blocks = cut_along(x, split_dim, devices)
+    outs = [blocks[index]]
+    for step in range(1, devices):
+        sent = blocks[index ^ step]
+        outs.append(lax.ppermute(sent, axis, [(i, i ^ step) for i in range(devices)]))
+    blocks = jnp.stack(outs)[index ^ jnp.arange(devices)]
+    return joined_along(blocks, concat_dim)
 
 
 def partner(value, axis, apart):
@@ -141,7 +163,7 @@
     returned = (
         lax.all_to_all(to_tokens(query_grad), "seq", split_axis=0, concat_axis=2, tiled=True),
         lax.all_to_all(to_tokens(key_grad), "seq", split_axis=0, concat_axis=2, tiled=True),
-        lax.all_to_all(to_tokens(value_grad), "seq", split_axis=0, concat_axis=2, tiled=True),
+        pairwise_exchange(to_tokens(value_grad), "seq", 0, 2),
     )
     return (from_heads(returned[0]), from_heads(returned[1]), from_heads(returned[2]), weight_grad)
 

time: 258 us -> 247 us (0.957)
  blocking collectives: 19.9 us -> 0 us
  starting transfers between devices: 32.3 us -> 42 us
    all_to_all x1 -> x0, blocking collectives: 19.9 us -> none  [body(): lax.all_to_all(to_tokens(key_grad), 'seq', split_axis=0, concat_axis=2, t...]
    ppermute x0 -> x7, starting transfers between devices: none -> 8.44 us  [pairwise_exchange(): lax.ppermute(sent, axis, [(i, i ^ step) for i in range(devices)])]
    unnamed x60 -> x70, local copies, waits for them, and re-layouts: 6.83 us -> 5.24 us
  transfers between devices with their start and end apart: 13 -> 20, of which waited for: 5 -> 6; matrix products, arithmetic and copies ran while one was open for 48% -> 50% of each run, Pallas kernels for 0% -> 0%
where the time goes in v1:
time: 247 us; the launch traced here: 245 us
  waiting for transfers between devices  61.9 us (25%)
  local copies, waits for them, and re-layouts  59.5 us (24%)
  matrix products  44.2 us (18%)
  starting transfers between devices  42 us (17%)
  other arithmetic  22.3 us (9%)
  between operations  14.6 us (6%)
    all_to_all x1, waiting for transfers between devices, body(): lax.all_to_all(to_heads(values), 'seq', split_axis=1, concat_axis=0, tile...  14 us
    all_to_all x1, waiting for transfers between devices, body(): lax.all_to_all(to_heads(out_grad), 'seq', split_axis=1, concat_axis=0, ti...  13.9 us
    all_to_all x1, waiting for transfers between devices, body(): lax.all_to_all(to_heads(key_vectors), 'seq', split_axis=1, concat_axis=0,...  12.6 us
    all_to_all x1, waiting for transfers between devices, body(): lax.all_to_all(to_heads(queries), 'seq', split_axis=1, concat_axis=0, til...  10.9 us
    dot_general x4, matrix products, body(): jnp.einsum('hqk,khd->qhd', dscore, key_block, preferred_element_type=jnp....  10.4 us
    dot_general x4, matrix products, body(): jnp.einsum('hqk,qhd->khd', dscore, query_block, preferred_element_type=jn...  10.4 us
    dot_general x4, matrix products, body(): jnp.einsum('hqk,qhd->khd', probs_low, grad_block, preferred_element_type=...  9.57 us
    all_to_all x1, waiting for transfers between devices, body(): lax.all_to_all(to_tokens(key_grad), 'seq', split_axis=0, concat_axis=2, t...  9.14 us
  transfers between devices with their start and end apart: 20, of which 6 were waited for; matrix products, arithmetic and copies ran while one was open for 50% of the time, Pallas kernels for 0%

profile of v1, /device:TPU:0, one launch (start us, length us, event | category | flops | bytes accessed | tf_op | source)
XLA Modules:
  0.0 244.6 jit_solution(12995271659172889130)
XLA Ops:
  9.6 6.5 %all-to-all-start.2 = ((bf16[64,8,512]{2,0,1:T(8,128)(2,1)}), bf16[64,8,512]{2,0,1:T(8,128)(2,1)S(1)}, u32[]{:S(2)}, u32[]{:S(2)}) async-start(bf16[64,8,512]{2,0,1:T(8,128)(2,1)} %bitcast.15), calls=%async_computation.2 | async-start | bytes 1048576 | tf_op jit(solution)/shard_map/all_to_all | solution.py:64
  17.4 14.0 %all-to-all-done.2 = bf16[64,8,512]{2,0,1:T(8,128)(2,1)S(1)} async-done(((bf16[64,8,512]{2,0,1:T(8,128)(2,1)}), bf16[64,8,512]{2,0,1:T(8,128)(2,1)S(1)}, u32[]{:S(2)}, u32[]{:S(2)}) %all-to-all-start.2) | async-done | bytes 524320 | tf_op jit(solution)/shard_map/all_to_all | solution.py:64
  31.4 3.6 %all-to-all-start.3 = ((bf16[64,8,512]{2,0,1:T(8,128)(2,1)}), bf16[64,8,512]{2,0,1:T(8,128)(2,1)S(1)}, u32[]{:S(2)}, u32[]{:S(2)}) async-start(bf16[64,8,512]{2,0,1:T(8,128)(2,1)} %bitcast.24), calls=%async_computation.3 | async-start | bytes 1048576 | tf_op jit(solution)/shard_map/all_to_all | solution.py:65
  36.4 13.9 %all-to-all-done.3 = bf16[64,8,512]{2,0,1:T(8,128)(2,1)S(1)} async-done(((bf16[64,8,512]{2,0,1:T(8,128)(2,1)}), bf16[64,8,512]{2,0,1:T(8,128)(2,1)S(1)}, u32[]{:S(2)}, u32[]{:S(2)}) %all-to-all-start.3) | async-done | bytes 524320 | tf_op jit(solution)/shard_map/all_to_all | solution.py:65
  50.4 3.5 %all-to-all-start = ((bf16[64,8,512]{2,0,1:T(8,128)(2,1)}), bf16[64,8,512]{2,0,1:T(8,128)(2,1)S(1)}, u32[]{:S(2)}, u32[]{:S(2)}) async-start(bf16[64,8,512]{2,0,1:T(8,128)(2,1)} %bitcast.1), calls=%async_computation | async-start | bytes 1048576 | tf_op jit(solution)/shard_map/all_to_all | solution.py:63
  56.6 12.6 %all-to-all-done = bf16[64,8,512]{2,0,1:T(8,128)(2,1)S(1)} async-done(((bf16[64,8,512]{2,0,1:T(8,128)(2,1)}), bf16[64,8,512]{2,0,1:T(8,128)(2,1)S(1)}, u32[]{:S(2)}, u32[]{:S(2)}) %all-to-all-start) | async-done | bytes 524320 | tf_op jit(solution)/shard_map/all_to_all | solution.py:63
  69.1 3.5 %all-to-all-start.1 = ((bf16[64,8,512]{2,0,1:T(8,128)(2,1)}), bf16[64,8,512]{2,0,1:T(8,128)(2,1)S(1)}, u32[]{:S(2)}, u32[]{:S(2)}) async-start(bf16[64,8,512]{2,0,1:T(8,128)(2,1)} %bitcast.10), calls=%async_computation.1 | async-start | bytes 1048576 | tf_op jit(solution)/shard_map/all_to_all | solution.py:62
  77.0 10.9 %all-to-all-done.1 = bf16[64,8,512]{2,0,1:T(8,128)(2,1)S(1)} async-done(((bf16[64,8,512]{2,0,1:T(8,128)(2,1)}), bf16[64,8,512]{2,0,1:T(8,128)(2,1)S(1)}, u32[]{:S(2)}, u32[]{:S(2)}) %all-to-all-start.1) | async-done | bytes 524320 | tf_op jit(solution)/shard_map/all_to_all | solution.py:62
  89.5 3.8 %all-to-all-start.6 = ((bf16[64,8,2048]{2,0,1:T(8,128)(2,1)}), bf16[64,8,2048]{2,0,1:T(8,128)(2,1)S(1)}, u32[]{:S(2)}, u32[]{:S(2)}) async-start(bf16[64,8,2048]{2,0,1:T(8,128)(2,1)} %bitcast.80), calls=%async_computation.6 | async-start | bytes 4194304 | tf_op jit(solution)/shard_map/all_to_all | solution.py:140
  112.3 2.3 convolution_bitcast_fusion.3
  114.6 2.5 %scatter-add.34 = f32[1024,4,128]{2,0,1:T(8,128)} pad(f32[256,4,128]{2,0,1:T(8,128)} %convolution_bitcast_fusion.3, f32[]{:T(128)} %constant.225.clone.1), padding=0_768x0_0x0_0 | pad | bytes 2621444 | tf_op jit(solution)/shard_map/scatter-add | solution.py:119
  121.4 2.4 fusion.17
  126.2 2.4 fusion.24
  133.7 2.5 %fusion.26 = f32[1024,4,128]{2,0,1:T(8,128)} fusion(f32[1024,4,128]{2,0,1:T(8,128)} %fusion.24, bf16[128,4,128]{2,1,0:T(4,128)(2,1)S(1)} %slice.333, f32[4,128]{1,0:T(4,128)S(1)} %get-tuple-element.134, pred[128,256]{0,1:T(8,128)(4,1)} %broadcast_compare_fusion, bf16[256,4,128]{2,1,0:T(4,128)(2,1)} %slice.327, bf16[128,4,128]{2,1,0:T(4,128)(2,1)} %slice.329), kind=kOutput, calls=%fused_computation.57 | convolution fusion | flops 67896064 | bytes 1607680 | tf_op jit(solution)/shard_map/hqk,qhd->khd/dot_general | solution.py:120
  136.2 3.9 %copy.167 = bf16[1024,4,128]{2,1,0:T(4,128)(2,1)} copy(f32[1024,4,128]{2,0,1:T(8,128)} %fusion.26) | data formatting | bytes 3145728 | tf_op jit(solution)/shard_map/scatter-add | solution.py:119
  141.6 3.0 %fusion.60 = (bf16[512,1,512]{2,1,0:T(2,128)(2,1)S(1)}, f32[512,1,512]{2,1,0:T(1,128)}) fusion(pred[]{:T(512)S(6)} %eq.5, bf16[512,2,512]{2,1,0:T(2,128)(2,1)S(1)} %reshape.507), kind=kLoop, calls=%fused_computation.99 | loop fusion | flops 786432 | bytes 2621441 | tf_op jit(solution)/shard_map/convert_element_type | solution.py:128
  146.1 2.6 %fusion.54 = bf16[128,4,128]{2,0,1:T(8,128)(2,1)} fusion(f32[4,128,256]{1,2,0:T(8,128)} %convolution_bitcast_fusion.8, bf16[256,4,128]{2,1,0:T(4,128)(2,1)S(1)} %copy-done.17, f32[4,128,256]{1,2,0:T(8,128)} %get-tuple-element.135, f32[4,128]{1,0:T(4,128)S(1)} %get-tuple-element.134), kind=kOutput, calls=%fused_computation.93 | convolution fusion | flops 34538240 | bytes 1443840 | tf_op jit(solution)/shard_map/hqk,khd->qhd/dot_general | solution.py:112
  150.7 2.7 %fusion.53 = bf16[128,4,128]{2,0,1:T(8,128)(2,1)} fusion(f32[4,128,256]{1,2,0:T(8,128)} %convolution_bitcast_fusion.9, bf16[256,4,128]{2,1,0:T(4,128)(2,1)} %copy-done.18, f32[4,128,256]{1,2,0:T(8,128)} %get-tuple-element.137, f32[4,128]{1,0:T(4,128)S(1)} %get-tuple-element.136), kind=kOutput, calls=%fused_computation.92 | convolution fusion | flops 34538240 | bytes 1443840 | tf_op jit(solution)/shard_map/hqk,khd->qhd/dot_general | solution.py:112
  154.4 2.6 %fusion.52 = bf16[128,4,128]{2,0,1:T(8,128)(2,1)} fusion(f32[4,128,256]{1,2,0:T(8,128)} %convolution_bitcast_fusion.10, bf16[256,4,128]{2,1,0:T(4,128)(2,1)} %slice.311, f32[4,128,256]{1,2,0:T(8,128)} %get-tuple-element.139, f32[4,128]{1,0:T(4,128)S(1)} %copy-done.28), kind=kOutput, calls=%fused_computation.91 | convolution fusion | flops 34538240 | bytes 1443840 | tf_op jit(solution)/shard_map/hqk,khd->qhd/dot_general | solution.py:112
  157.3 2.5 %fusion.51 = bf16[128,4,128]{2,0,1:T(8,128)(2,1)} fusion(f32[4,128,256]{1,2,0:T(8,128)S(1)} %convolution_bitcast_fusion.11, bf16[256,4,128]{2,1,0:T(4,128)(2,1)} %copy-done.16, f32[4,128,256]{1,2,0:T(8,128)} %get-tuple-element.141, f32[4,128]{1,0:T(4,128)S(1)} %get-tuple-element.140), kind=kOutput, calls=%fused_computation.90 | convolution fusion | flops 34538240 | bytes 1443840 | tf_op jit(solution)/shard_map/hqk,khd->qhd/dot_general | solution.py:112
  165.7 2.7 %fusion.18 = f32[1024,4,128]{2,0,1:T(8,128)} fusion(f32[1024,4,128]{2,0,1:T(8,128)} %scatter-add.26, f32[4,128,256]{1,2,0:T(8,128)} %convolution_bitcast_fusion.10, bf16[128,4,128]{2,1,0:T(4,128)(2,1)S(1)} %copy-done.23, f32[4,128,256]{1,2,0:T(8,128)} %get-tuple-element.139, f32[4,128]{1,0:T(4,128)S(1)} %copy-done.29), kind=kOutput, calls=%fused_computation.44 | convolution fusion | flops 34472704 | bytes 2756608 | tf_op jit(solution)/shard_map/hqk,qhd->khd/dot_general | solution.py:117
  169.9 4.8 %all-to-all-start.4 = ((bf16[8,64,1,512]{3,1,2,0:T(8,128)(2,1)}), bf16[8,64,1,512]{3,1,2,0:T(8,128)(2,1)}, u32[]{:S(2)}, u32[]{:S(2)}) async-start(bf16[8,64,1,512]{3,1,2,0:T(8,128)(2,1)} %bitcast.40), calls=%async_computation.4 | async-start | bytes 1048576 | tf_op jit(solution)/shard_map/all_to_all | solution.py:164
  180.2 2.9 %copy.180 = f32[2048,1,256]{2,0,1:T(8,128)} copy(f32[2048,1,256]{0,2,1:T(8,128)} %get-tuple-element.100) | data formatting | bytes 4194304
  186.4 2.9 %fusion.20 = f32[1024,4,128]{2,0,1:T(8,128)} fusion(f32[1024,4,128]{2,0,1:T(8,128)} %fusion.18, f32[4,128,256]{1,2,0:T(8,128)} %convolution_bitcast_fusion.9, bf16[128,4,128]{2,1,0:T(4,128)(2,1)S(1)} %copy-done.22, f32[4,128,256]{1,2,0:T(8,128)} %get-tuple-element.137, f32[4,128]{1,0:T(4,128)S(1)} %get-tuple-element.136), kind=kOutput, calls=%fused_computation.51 | convolution fusion | flops 34603776 | bytes 3280896 | tf_op jit(solution)/shard_map/hqk,qhd->khd/dot_general | solution.py:117
  189.3 2.9 %fusion.22 = f32[1024,4,128]{2,0,1:T(8,128)} fusion(f32[1024,4,128]{2,0,1:T(8,128)} %fusion.20, f32[4,128,256]{1,2,0:T(8,128)} %convolution_bitcast_fusion.8, bf16[128,4,128]{2,1,0:T(4,128)(2,1)S(1)} %copy-done.20, f32[4,128,256]{1,2,0:T(8,128)} %get-tuple-element.135, f32[4,128]{1,0:T(4,128)S(1)} %get-tuple-element.134), kind=kOutput, calls=%fused_computation.53 | convolution fusion | flops 34603776 | bytes 3280896 | tf_op jit(solution)/shard_map/hqk,qhd->khd/dot_general | solution.py:117
  192.2 3.9 %copy.160 = bf16[1024,4,128]{2,1,0:T(4,128)(2,1)} copy(f32[1024,4,128]{2,0,1:T(8,128)} %fusion.22) | data formatting | bytes 3145728 | tf_op jit(solution)/shard_map/scatter-add | solution.py:116
  197.6 3.0 %fusion.57 = (bf16[512,1,512]{2,1,0:T(2,128)(2,1)S(1)}, f32[512,1,512]{2,1,0:T(1,128)}) fusion(pred[]{:T(512)S(6)} %eq.5, bf16[512,2,512]{2,1,0:T(2,128)(2,1)S(1)} %reshape.503), kind=kLoop, calls=%fused_computation.96 | loop fusion | flops 786432 | bytes 2621441 | tf_op jit(solution)/shard_map/convert_element_type | solution.py:128
  200.9 2.7 %fusion.8 = bf16[2048,256]{1,0:T(8,128)(2,1)} fusion(bf16[2048,256]{1,0:T(8,128)(2,1)} %collective-permute-done.11, f32[2048,1,256]{2,0,1:T(8,128)S(1)} %copy-done, f32[2048,1,256]{2,0,1:T(8,128)S(1)} %copy.181, pred[]{:T(512)S(6)} %eq.5), kind=kLoop, calls=%fused_computation.10 | loop fusion | flops 2097152 | bytes 6291457 | tf_op jit(solution)/shard_map/convert_element_type | solution.py:150
  205.8 2.4 collective-permute-start.7
  210.6 3.5 %collective-permute-start.9 = (bf16[1,64,1,512]{3,1,2,0:T(8,128)(2,1)S(1)}, bf16[1,64,1,512]{3,1,2,0:T(8,128)(2,1)S(1)}, u32[]{:S(2)}, u32[]{:S(2)}) collective-permute-start(bf16[1,64,1,512]{3,1,2,0:T(8,128)(2,1)S(1)} %get-tuple-element.119), channel_id=1, source_target_pairs={{0,6},{1,7},{2,4},{3,5},{4,2},{5,3},{6,0},{7,1},{8,14},{9,15},{10,... | collective-permute-start | bytes 196616 | tf_op jit(solution)/shard_map/ppermute | solution.py:26
  214.2 4.8 %all-to-all-start.5 = ((bf16[8,64,1,512]{3,1,2,0:T(8,128)(2,1)}), bf16[8,64,1,512]{3,1,2,0:T(8,128)(2,1)S(1)}, u32[]{:S(2)}, u32[]{:S(2)}) async-start(bf16[8,64,1,512]{3,1,2,0:T(8,128)(2,1)} %bitcast.50), calls=%async_computation.5 | async-start | bytes 1048576 | tf_op jit(solution)/shard_map/all_to_all | solution.py:165
  225.2 9.1 %all-to-all-done.5 = bf16[8,64,1,512]{3,1,2,0:T(8,128)(2,1)S(1)} async-done(((bf16[8,64,1,512]{3,1,2,0:T(8,128)(2,1)}), bf16[8,64,1,512]{3,1,2,0:T(8,128)(2,1)S(1)}, u32[]{:S(2)}, u32[]{:S(2)}) %all-to-all-start.5) | async-done | bytes 524320 | tf_op jit(solution)/shard_map/all_to_all | solution.py:165
  (178 shorter events, 82.7 us)
Async XLA Ops:
  7.2 8.9 %copy-start.13 = (bf16[1,128,2048]{2,1,0:T(8,128)(2,1)S(1)}, bf16[1,128,2048]{2,1,0:T(8,128)(2,1)}, u32[]{:S(2)}) copy-start(bf16[1,128,2048]{2,1,0:T(8,128)(2,1)} %param.24) | copy-start | bytes 1572868
  9.6 25.5 %copy-start.14 = (bf16[1,128,2048]{2,1,0:T(8,128)(2,1)S(1)}, bf16[1,128,2048]{2,1,0:T(8,128)(2,1)}, u32[]{:S(2)}) copy-start(bf16[1,128,2048]{2,1,0:T(8,128)(2,1)} %param.22) | copy-start | bytes 1572868
  9.6 21.8 %all-to-all-start.2 = ((bf16[64,8,512]{2,0,1:T(8,128)(2,1)}), bf16[64,8,512]{2,0,1:T(8,128)(2,1)S(1)}, u32[]{:S(2)}, u32[]{:S(2)}) async-start(bf16[64,8,512]{2,0,1:T(8,128)(2,1)} %bitcast.15), calls=%async_computation.2 | async-start | bytes 1048576 | tf_op jit(solution)/shard_map/all_to_all | solution.py:64
  31.4 22.4 %copy-start.15 = (bf16[1,128,2048]{2,1,0:T(8,128)(2,1)S(1)}, bf16[1,128,2048]{2,1,0:T(8,128)(2,1)}, u32[]{:S(2)}) copy-start(bf16[1,128,2048]{2,1,0:T(8,128)(2,1)} %param.21) | copy-start | bytes 1572868
  31.4 18.9 %all-to-all-start.3 = ((bf16[64,8,512]{2,0,1:T(8,128)(2,1)}), bf16[64,8,512]{2,0,1:T(8,128)(2,1)S(1)}, u32[]{:S(2)}, u32[]{:S(2)}) async-start(bf16[64,8,512]{2,0,1:T(8,128)(2,1)} %bitcast.24), calls=%async_computation.3 | async-start | bytes 1048576 | tf_op jit(solution)/shard_map/all_to_all | solution.py:65
  50.4 18.8 %all-to-all-start = ((bf16[64,8,512]{2,0,1:T(8,128)(2,1)}), bf16[64,8,512]{2,0,1:T(8,128)(2,1)S(1)}, u32[]{:S(2)}, u32[]{:S(2)}) async-start(bf16[64,8,512]{2,0,1:T(8,128)(2,1)} %bitcast.1), calls=%async_computation | async-start | bytes 1048576 | tf_op jit(solution)/shard_map/all_to_all | solution.py:63
  69.1 18.8 %all-to-all-start.1 = ((bf16[64,8,512]{2,0,1:T(8,128)(2,1)}), bf16[64,8,512]{2,0,1:T(8,128)(2,1)S(1)}, u32[]{:S(2)}, u32[]{:S(2)}) async-start(bf16[64,8,512]{2,0,1:T(8,128)(2,1)} %bitcast.10), calls=%async_computation.1 | async-start | bytes 1048576 | tf_op jit(solution)/shard_map/all_to_all | solution.py:62
  74.1 30.5 %collective-permute-start = (bf16[512,512]{1,0:T(8,128)(2,1)S(1)}, bf16[512,512]{1,0:T(8,128)(2,1)}, u32[]{:S(2)}, u32[]{:S(2)}) collective-permute-start(bf16[512,512]{1,0:T(8,128)(2,1)S(1)} %bitcast.268), channel_id=1, source_target_pairs={{0,1},{1,0},{2,3},{3,2},{4,5},{5,4},{6,7},{7,6},{8,9},{9,8},{10,11... | collective-permute-start | bytes 1572872 | tf_op jit(solution)/shard_map/ppermute | solution.py:32
  76.1 52.5 %collective-permute-start.1 = (bf16[512,512]{1,0:T(8,128)(2,1)S(1)}, bf16[512,512]{1,0:T(8,128)(2,1)}, u32[]{:S(2)}, u32[]{:S(2)}) collective-permute-start(bf16[512,512]{1,0:T(8,128)(2,1)S(1)} %bitcast.267), channel_id=1, source_target_pairs={{0,1},{1,0},{2,3},{3,2},{4,5},{5,4},{6,7},{7,6},{8,9},{9,8},{10,11... | collective-permute-start | bytes 1572872 | tf_op jit(solution)/shard_map/ppermute | solution.py:32
  89.5 80.4 %all-to-all-start.6 = ((bf16[64,8,2048]{2,0,1:T(8,128)(2,1)}), bf16[64,8,2048]{2,0,1:T(8,128)(2,1)S(1)}, u32[]{:S(2)}, u32[]{:S(2)}) async-start(bf16[64,8,2048]{2,0,1:T(8,128)(2,1)} %bitcast.80), calls=%async_computation.6 | async-start | bytes 4194304 | tf_op jit(solution)/shard_map/all_to_all | solution.py:140
  110.2 6.9 %copy-start.16 = (bf16[256,4,128]{2,1,0:T(4,128)(2,1)}, bf16[256,4,128]{2,1,0:T(4,128)(2,1)S(1)}, u32[]{:S(2)}) copy-start(bf16[256,4,128]{2,1,0:T(4,128)(2,1)S(1)} %slice.303) | copy-start | bytes 786436
  112.3 4.8 %copy-start.19 = (bf16[128,4,128]{2,1,0:T(4,128)(2,1)S(1)}, bf16[128,4,128]{2,1,0:T(4,128)(2,1)}, u32[]{:S(2)}) copy-start(bf16[128,4,128]{2,1,0:T(4,128)(2,1)} %slice.329) | copy-start | bytes 393220
  117.1 4.3 %copy-start.10 = (bf16[128,4,128]{2,1,0:T(4,128)(2,1)S(1)}, bf16[128,4,128]{2,1,0:T(4,128)(2,1)}, u32[]{:S(2)}) copy-start(bf16[128,4,128]{2,1,0:T(4,128)(2,1)} %slice.317) | copy-start | bytes 393220
  121.4 4.8 %copy-start.12 = (bf16[128,4,128]{2,1,0:T(4,128)(2,1)S(1)}, bf16[128,4,128]{2,1,0:T(4,128)(2,1)}, u32[]{:S(2)}) copy-start(bf16[128,4,128]{2,1,0:T(4,128)(2,1)} %slice.325) | copy-start | bytes 393220
  124.3 4.3 %copy-start.18 = (bf16[256,4,128]{2,1,0:T(4,128)(2,1)}, bf16[256,4,128]{2,1,0:T(4,128)(2,1)S(1)}, u32[]{:S(2)}) copy-start(bf16[256,4,128]{2,1,0:T(4,128)(2,1)S(1)} %slice.319) | copy-start | bytes 786436
  144.8 23.6 %collective-permute-start.3 = (bf16[512,512]{1,0:T(8,128)(2,1)S(1)}, bf16[512,512]{1,0:T(8,128)(2,1)}, u32[]{:S(2)}, u32[]{:S(2)}) collective-permute-start(bf16[512,512]{1,0:T(8,128)(2,1)S(1)} %bitcast.279), channel_id=1, source_target_pairs={{0,1},{1,0},{2,3},{3,2},{4,5},{5,4},{6,7},{7,6},{8,9},{9,8},{10,11... | collective-permute-start | bytes 1572872 | tf_op jit(solution)/shard_map/ppermute | solution.py:32
  148.7 4.7 %copy-start.5 = (bf16[256,4,128]{2,1,0:T(4,128)(2,1)S(1)}, bf16[256,4,128]{2,1,0:T(4,128)(2,1)}, u32[]{:S(2)}) copy-start(bf16[256,4,128]{2,1,0:T(4,128)(2,1)} %slice.315) | copy-start | bytes 786436
  169.9 6.1 %copy-start.1 = (bf16[512,512]{1,0:T(8,128)(2,1)}, bf16[512,512]{1,0:T(8,128)(2,1)S(1)}, u32[]{:S(2)}) copy-start(bf16[512,512]{1,0:T(8,128)(2,1)S(1)} %fusion.62) | copy-start | bytes 1572868
  169.9 44.2 %all-to-all-start.4 = ((bf16[8,64,1,512]{3,1,2,0:T(8,128)(2,1)}), bf16[8,64,1,512]{3,1,2,0:T(8,128)(2,1)}, u32[]{:S(2)}, u32[]{:S(2)}) async-start(bf16[8,64,1,512]{3,1,2,0:T(8,128)(2,1)} %bitcast.40), calls=%async_computation.4 | async-start | bytes 1048576 | tf_op jit(solution)/shard_map/all_to_all | solution.py:164
  174.7 61.2 %reduce-scatter.2.cloned.1.call-start = ((), (), s32[]{:S(2)}) async-start(), calls=%async_computation.8 | async-start | bytes 1310720 | tf_op jit(solution)/shard_map/reduce_scatter | solution.py:149
  184.4 4.9 %copy-start.20 = (bf16[128,4,128]{2,1,0:T(4,128)(2,1)S(1)}, bf16[128,4,128]{2,1,0:T(4,128)(2,1)}, u32[]{:S(2)}) copy-start(bf16[128,4,128]{2,1,0:T(4,128)(2,1)} %slice.329) | copy-start | bytes 393220
  184.4 16.5 %collective-permute-start.11 = (bf16[2048,256]{1,0:T(8,128)(2,1)}, bf16[2048,256]{1,0:T(8,128)(2,1)}, u32[]{:S(2)}, u32[]{:S(2)}) collective-permute-start(bf16[2048,256]{1,0:T(8,128)(2,1)} %fusion.61), channel_id=1, source_target_pairs={{0,1},{1,0},{2,3},{3,2},{4,5},{5,4},{6,7},{7,6},{8,9},{9,8},{10,11... | collective-permute-start | bytes 3145736 | tf_op jit(solution)/shard_map/ppermute | solution.py:32
  200.8 7.5 %collective-permute-start.2 = (bf16[512,512]{1,0:T(8,128)(2,1)S(1)}, bf16[512,512]{1,0:T(8,128)(2,1)}, u32[]{:S(2)}, u32[]{:S(2)}) collective-permute-start(bf16[512,512]{1,0:T(8,128)(2,1)S(1)} %bitcast.278), channel_id=1, source_target_pairs={{0,1},{1,0},{2,3},{3,2},{4,5},{5,4},{6,7},{7,6},{8,9},{9,8},{10,11... | collective-permute-start | bytes 1572872 | tf_op jit(solution)/shard_map/ppermute | solution.py:32
  203.6 5.0 %copy-start.3 = (f32[512,1,512]{2,1,0:T(1,128)S(1)}, f32[512,1,512]{2,1,0:T(1,128)}, u32[]{:S(2)}) copy-start(f32[512,1,512]{2,1,0:T(1,128)} %get-tuple-element.105) | copy-start | bytes 3145732
  203.7 6.9 %collective-permute-start.4 = (bf16[1,64,1,512]{3,1,2,0:T(8,128)(2,1)S(1)}, bf16[1,64,1,512]{3,1,2,0:T(8,128)(2,1)S(1)}, u32[]{:S(2)}, u32[]{:S(2)}) collective-permute-start(bf16[1,64,1,512]{3,1,2,0:T(8,128)(2,1)S(1)} %get-tuple-element.124), channel_id=1, source_target_pairs={{0,1},{1,0},{2,3},{3,2},{4,5},{5,4},{6,7},{7,6},{8,9},{9,8},{10,11... | collective-permute-start | bytes 196616 | tf_op jit(solution)/shard_map/ppermute | solution.py:26
  204.2 9.9 %collective-permute-start.5 = (bf16[1,64,1,512]{3,1,2,0:T(8,128)(2,1)S(1)}, bf16[1,64,1,512]{3,1,2,0:T(8,128)(2,1)S(1)}, u32[]{:S(2)}, u32[]{:S(2)}) collective-permute-start(bf16[1,64,1,512]{3,1,2,0:T(8,128)(2,1)S(1)} %get-tuple-element.123), channel_id=1, source_target_pairs={{0,2},{1,3},{2,0},{3,1},{4,6},{5,7},{6,4},{7,5},{8,10},{9,11},{10,... | collective-permute-start | bytes 196616 | tf_op jit(solution)/shard_map/ppermute | solution.py:26
  205.8 13.2 %collective-permute-start.6 = (bf16[1,64,1,512]{3,1,2,0:T(8,128)(2,1)S(1)}, bf16[1,64,1,512]{3,1,2,0:T(8,128)(2,1)S(1)}, u32[]{:S(2)}, u32[]{:S(2)}) collective-permute-start(bf16[1,64,1,512]{3,1,2,0:T(8,128)(2,1)S(1)} %get-tuple-element.122), channel_id=1, source_target_pairs={{0,3},{1,2},{2,1},{3,0},{4,7},{5,6},{6,5},{7,4},{8,11},{9,10},{10,... | collective-permute-start | bytes 196616 | tf_op jit(solution)/shard_map/ppermute | solution.py:26
  205.8 13.2 %collective-permute-start.7 = (bf16[1,64,1,512]{3,1,2,0:T(8,128)(2,1)S(1)}, bf16[1,64,1,512]{3,1,2,0:T(8,128)(2,1)S(1)}, u32[]{:S(2)}, u32[]{:S(2)}) collective-permute-start(bf16[1,64,1,512]{3,1,2,0:T(8,128)(2,1)S(1)} %get-tuple-element.121), channel_id=1, source_target_pairs={{0,4},{1,5},{2,6},{3,7},{4,0},{5,1},{6,2},{7,3},{8,12},{9,13},{10,... | collective-permute-start | bytes 196616 | tf_op jit(solution)/shard_map/ppermute | solution.py:26
  208.2 10.8 %collective-permute-start.8 = (bf16[1,64,1,512]{3,1,2,0:T(8,128)(2,1)S(1)}, bf16[1,64,1,512]{3,1,2,0:T(8,128)(2,1)S(1)}, u32[]{:S(2)}, u32[]{:S(2)}) collective-permute-start(bf16[1,64,1,512]{3,1,2,0:T(8,128)(2,1)S(1)} %get-tuple-element.120), channel_id=1, source_target_pairs={{0,5},{1,4},{2,7},{3,6},{4,1},{5,0},{6,3},{7,2},{8,13},{9,12},{10,... | collective-permute-start | bytes 196616 | tf_op jit(solution)/shard_map/ppermute | solution.py:26
  210.6 8.5 %collective-permute-start.9 = (bf16[1,64,1,512]{3,1,2,0:T(8,128)(2,1)S(1)}, bf16[1,64,1,512]{3,1,2,0:T(8,128)(2,1)S(1)}, u32[]{:S(2)}, u32[]{:S(2)}) collective-permute-start(bf16[1,64,1,512]{3,1,2,0:T(8,128)(2,1)S(1)} %get-tuple-element.119), channel_id=1, source_target_pairs={{0,6},{1,7},{2,4},{3,5},{4,2},{5,3},{6,0},{7,1},{8,14},{9,15},{10,... | collective-permute-start | bytes 196616 | tf_op jit(solution)/shard_map/ppermute | solution.py:26
  214.1 6.3 %collective-permute-start.10 = (bf16[1,64,1,512]{3,1,2,0:T(8,128)(2,1)S(1)}, bf16[1,64,1,512]{3,1,2,0:T(8,128)(2,1)S(1)}, u32[]{:S(2)}, u32[]{:S(2)}) collective-permute-start(bf16[1,64,1,512]{3,1,2,0:T(8,128)(2,1)S(1)} %get-tuple-element.118), channel_id=1, source_target_pairs={{0,7},{1,6},{2,5},{3,4},{4,3},{5,2},{6,1},{7,0},{8,15},{9,14},{10,... | collective-permute-start | bytes 196616 | tf_op jit(solution)/shard_map/ppermute | solution.py:26
  214.2 20.2 %all-to-all-start.5 = ((bf16[8,64,1,512]{3,1,2,0:T(8,128)(2,1)}), bf16[8,64,1,512]{3,1,2,0:T(8,128)(2,1)S(1)}, u32[]{:S(2)}, u32[]{:S(2)}) async-start(bf16[8,64,1,512]{3,1,2,0:T(8,128)(2,1)} %bitcast.50), calls=%async_computation.5 | async-start | bytes 1048576 | tf_op jit(solution)/shard_map/all_to_all | solution.py:165
  (18 other events, 52.5 us)
Sparse Core Ops, SparseCore 0:
  203.7 28.9 reduce-scatter.1
